TPU v7x, 256 devices: a whole 4x4x8 slice. The times are simulated.
256 devices in a mesh: ba: 8 (over z), aa: 32 (over x, y, core).
Axes of the slice: x: 4, y: 4, z: 8, core: 2. Of those that a mesh axis runs over, the one named last changes fastest.
Arguments:
- tokens: bfloat16 [49152, 1024], P(('ba', 'aa')), parts along dimension 0, may hold values from -6 to 6
- latents: bfloat16 [8192, 1024], P(('ba', 'aa')), parts along dimension 0, may hold values from -6 to 6
- read_query: bfloat16 [1024, 512], replicated, may hold values from -0.1875 to 0.1875
- read_keyval: bfloat16 [1024, 1024], replicated, may hold values from -0.1875 to 0.1875
- read_out: bfloat16 [512, 1024], replicated, may hold values from -0.25 to 0.25
- self_qkv: bfloat16 [1024, 1536], replicated, may hold values from -0.1875 to 0.1875
- self_out: bfloat16 [512, 1024], replicated, may hold values from -0.25 to 0.25
- write_query: bfloat16 [1024, 512], replicated, may hold values from -0.1875 to 0.1875
- write_keyval: bfloat16 [1024, 1024], replicated, may hold values from -0.1875 to 0.1875
- write_out: bfloat16 [512, 1024], replicated, may hold values from -0.25 to 0.25
- qk_gain: float32 [6, 512], replicated, may hold values from 0.8 to 2.2
Outputs:
- tokens_out: bfloat16 [49152, 1024], P(('ba', 'aa')), parts along dimension 0
- latents_out: bfloat16 [8192, 1024], P(('ba', 'aa')), parts along dimension 0
There are 8 independent parts, one for each index of `ba`. A program takes and returns all parts, laid end to end along the dimension named above; an argument that names none is the same for every part. Nothing has to cross between parts.
All inputs are finite; a program needn't handle non-finite values.
Results may differ from a plain program's by a relative error of at most 0.014.
Values may be sent and summed in bfloat16 or wider, within the bound.
No kernel may reach another device: no remote copies, remote signals or barrier semaphores. Data moves between devices by JAX's collectives and lax.ppermute only.
A program may use at most 64 MiB of HBM per device.

v0:
```python
import math

import jax
import jax.numpy as jnp
from jax import lax
from jax.sharding import Mesh
from jax.sharding import PartitionSpec as P

HEADS = 8
AA = ("aa_0", "aa_1", "aa_2")
BA_AA = ("ba", "aa_0", "aa_1", "aa_2")


EPSILON = 1e-06


def sent_to_all(x, axis):
    copies = jnp.broadcast_to(x, (lax.axis_size(axis), *x.shape))
    return lax.all_to_all(copies, axis, split_axis=0, concat_axis=0, tiled=True)


def laid_out(parts, dim):
    parts = jnp.moveaxis(parts, 0, dim)
    lengths = parts.shape
    return parts.reshape(*lengths[:dim], lengths[dim] * lengths[dim + 1], *lengths[dim + 2 :])


def collect(x, axis, dim):
    parts = sent_to_all(x, axis)
    return laid_out(parts, dim)


def in_blocks(x, dim, devices):
    lengths = x.shape
    parts = x.reshape(*lengths[:dim], devices, lengths[dim] // devices, *lengths[dim + 1 :])
    return jnp.moveaxis(parts, dim, 0)


def sent_and_summed(x, axis, dim):
    parts = in_blocks(x, dim, lax.axis_size(axis))
    arrived = lax.all_to_all(parts, axis, split_axis=0, concat_axis=0, tiled=True)
    return arrived.sum(axis=0)


def side_by_side(arrays, axis, dim, along):
    both = jnp.concatenate(arrays, axis=along)
    result, at, done = (sent_and_summed(both, axis, dim), 0, [])
    for a in arrays:
        done.append(lax.slice_in_dim(result, at, at + a.shape[along], axis=along))
        at += a.shape[along]
    return tuple(done)


def gathered_by_axis(x, axes, dim):
    far, near = axes
    parts = sent_to_all(sent_to_all(x, far), near)
    return laid_out(parts.swapaxes(0, 1).reshape(-1, *x.shape), dim)


def side_by_side_2(arrays, axis, dim, along):
    widths = [a.shape[along] for a in arrays]
    both = jnp.concatenate(arrays, axis=along)
    result = gathered_by_axis(both, axis, dim)
    return tuple(jnp.split(result, [sum(widths[:k]) for k in range(1, len(widths))], axis=along))


def rms_rows(values):
    widened = values.astype(jnp.float32)
    return (
        widened * lax.rsqrt(jnp.mean(widened * widened, axis=-1, keepdims=True) + EPSILON)
    ).astype(jnp.bfloat16)


def head_norm(projected, gain_row, head_count):
    row_count = projected.shape[0]
    split_heads = projected.reshape(row_count, head_count, -1)
    normed = split_heads * lax.rsqrt(
        jnp.mean(split_heads * split_heads, axis=-1, keepdims=True) + EPSILON
    )
    return (normed.reshape(row_count, -1) * gain_row).astype(jnp.bfloat16)


def attend_block(query_rows, key_rows, value_rows, head_count):
    row_count = query_rows.shape[0]
    query_heads = query_rows.reshape(row_count, head_count, -1)
    key_heads = key_rows.reshape(key_rows.shape[0], head_count, -1)
    value_heads = value_rows.reshape(value_rows.shape[0], head_count, -1)
    score_scale = 1.0 / math.sqrt(query_heads.shape[2])
    scores = (
        jnp.einsum("qhe,khe->hqk", query_heads, key_heads, preferred_element_type=jnp.float32)
        * score_scale
    )
    weights = jnp.exp(scores)
    denominator = jnp.sum(weights, axis=2).T
    numerator = jnp.einsum(
        "hqk,khe->qhe",
        weights.astype(jnp.bfloat16),
        value_heads,
        preferred_element_type=jnp.float32,
    )
    return (numerator.reshape(row_count, -1), denominator)


def partial_attend(query_rows, key_rows, value_rows, head_count):
    row_count = query_rows.shape[0]
    if row_count > 512 and row_count % 512 == 0:
        blocks = query_rows.reshape(row_count // 512, 512, query_rows.shape[1])
        numerator, denominator = lax.map(
            lambda one_block: attend_block(one_block, key_rows, value_rows, head_count), blocks
        )
        return (numerator.reshape(row_count, -1), denominator.reshape(row_count, head_count))
    return attend_block(query_rows, key_rows, value_rows, head_count)


def finish_heads(numerator, denominator, head_count):
    row_count = numerator.shape[0]
    quotient = numerator.reshape(row_count, head_count, -1) / denominator[:, :, None]
    return quotient.reshape(row_count, -1).astype(jnp.bfloat16)


def attention(query_rows, key_rows, value_rows, head_count):
    numerator, denominator = partial_attend(query_rows, key_rows, value_rows, head_count)
    return finish_heads(numerator, denominator, head_count)


def residual_add(base, attended, projection):
    update = jnp.dot(attended, projection, preferred_element_type=jnp.float32)
    return (base.astype(jnp.float32) + update).astype(jnp.bfloat16)


def self_block(read_latents, self_qkv, qk_gain, inner_width):
    triple = jnp.dot(rms_rows(read_latents), self_qkv, preferred_element_type=jnp.float32)
    self_queries = head_norm(triple[:, :inner_width], qk_gain[2], HEADS)
    self_keys = head_norm(triple[:, inner_width : 2 * inner_width], qk_gain[3], HEADS)
    self_values = triple[:, 2 * inner_width :].astype(jnp.bfloat16)
    return (self_queries, self_keys, self_values)


def write_pairs(latent_rows, write_keyval, qk_gain, inner_width):
    latent_pairs = jnp.dot(rms_rows(latent_rows), write_keyval, preferred_element_type=jnp.float32)
    write_keys = head_norm(latent_pairs[:, :inner_width], qk_gain[5], HEADS)
    write_values = latent_pairs[:, inner_width:].astype(jnp.bfloat16)
    return (write_keys, write_values)


def per_device(
    tokens,
    latents,
    read_query,
    read_keyval,
    read_out,
    self_qkv,
    self_out,
    write_query,
    write_keyval,
    write_out,
    qk_gain,
):
    inner_width = read_query.shape[1]
    normed_tokens = rms_rows(tokens)
    token_pairs = jnp.dot(normed_tokens, read_keyval, preferred_element_type=jnp.float32)
    read_keys = head_norm(token_pairs[:, :inner_width], qk_gain[1], HEADS)
    read_values = token_pairs[:, inner_width:].astype(jnp.bfloat16)
    own_queries = head_norm(
        jnp.dot(rms_rows(latents), read_query, preferred_element_type=jnp.float32),
        qk_gain[0],
        HEADS,
    )
    read_queries = collect(own_queries, AA, 0)
    numerator, denominator = partial_attend(read_queries, read_keys, read_values, HEADS)
    numerator, denominator = side_by_side((numerator, denominator), AA, 0, 1)
    own_read = residual_add(latents, finish_heads(numerator, denominator, HEADS), read_out)
    write_queries = head_norm(
        jnp.dot(normed_tokens, write_query, preferred_element_type=jnp.float32), qk_gain[4], HEADS
    )
    self_queries, own_keys, own_values = self_block(own_read, self_qkv, qk_gain, inner_width)
    self_keys, self_values = side_by_side_2(
        (own_keys, own_values), (("aa_0", "aa_1"), "aa_2"), 0, 1
    )
    self_attended = attention(self_queries, self_keys, self_values, HEADS)
    latents_out = residual_add(own_read, self_attended, self_out)
    own_wkeys, own_wvalues = write_pairs(latents_out, write_keyval, qk_gain, inner_width)
    write_keys, write_values = side_by_side_2(
        (own_wkeys, own_wvalues), (("aa_0", "aa_1"), "aa_2"), 0, 1
    )
    write_attended = attention(write_queries, write_keys, write_values, HEADS)
    tokens_out = residual_add(tokens, write_attended, write_out)
    return (tokens_out, latents_out)


def solution(mesh):
    torus = Mesh(mesh.devices.reshape(mesh.shape["ba"], 4, 4, 2), ("ba", "aa_0", "aa_1", "aa_2"))
    in_specs = (P(BA_AA, None), P(BA_AA, None), P(), P(), P(), P(), P(), P(), P(), P(), P())
    out_specs = (P(BA_AA, None), P(BA_AA, None))
    return jax.shard_map(
        per_device, mesh=torus, in_specs=in_specs, out_specs=out_specs, check_vma=False
    )
```

profile of v0, /device:TPU:1, one launch (start us, length us, event | category | flops | bytes accessed | tf_op | source)
XLA Modules:
  0.0 187.5 jit_solution(14653353147435164038)
XLA Ops:
  0.6 1.1 fusion.36
  1.8 1.6 fusion.52
  3.3 2.3 %fusion.53 = (f32[32,512]{1,0:T(8,128)}, f32[32,512]{1,0:T(8,128)}) fusion(bf16[1024,512]{1,0:T(8,128)(2,1)} %param.15, bf16[32,1024]{1,0:T(8,128)(2,1)} %param.14, f32[32]{0:T(128)S(1)} %add_rsqrt_fusion.9), kind=kOutput, calls=%fused_computation.87 | convolution fusion | flops 33669120 | bytes 1245312 | tf_op jit(solution)/shard_map/dot_general | solution.py:165
  5.6 1.6 mul.225
  7.2 1.0 reduce_sum.127
  8.2 0.8 mul.226
  9.0 1.6 mul.227
  10.6 0.9 multiply_convert_fusion.7
  11.5 1.1 broadcast_in_dim.44
  12.6 8.6 %all-to-all-start = ((bf16[32,32,512]{2,1,0:T(8,128)(2,1)}), bf16[32,32,512]{2,1,0:T(8,128)(2,1)}, u32[]{:S(2)}, u32[]{:S(2)}) async-start(bf16[32,32,512]{2,1,0:T(8,128)(2,1)} %broadcast_in_dim.44), calls=%async_computation | async-start | bytes 2097152 | tf_op jit(solution)/shard_map/all_to_all | solution.py:19
  21.5 2.2 %fusion.32 = f32[192,1024]{1,0:T(8,128)S(1)} fusion(bf16[1024,1024]{1,0:T(8,128)(2,1)} %param.16, bf16[192,1024]{1,0:T(8,128)(2,1)S(1)} %copy-done.2, f32[192]{0:T(256)S(1)} %add_rsqrt_fusion.6), kind=kOutput, calls=%fused_computation.46 | convolution fusion | flops 403243008 | bytes 3277568 | tf_op jit(solution)/shard_map/dot_general | solution.py:161
  23.7 0.9 copy-done.5
  24.6 0.7 slice.87
  25.3 1.1 copy.40
  26.3 1.8 slice_multiply_fusion
  28.1 2.0 %copy.36 = f32[192,512]{0,1:T(8,128)} copy(f32[192,512]{1,0:T(8,128)} %slice_multiply_fusion) | data formatting | bytes 786432 | tf_op jit(solution)/shard_map/mul | solution.py:78
  30.1 1.1 bitcast_reduce_fusion.1
  31.2 0.8 mul.237
  32.1 2.0 %copy.37 = f32[192,512]{1,0:T(8,128)} copy(f32[192,512]{0,1:T(8,128)} %bitcast.96) | data formatting | bytes 786432 | tf_op jit(solution)/shard_map/mul | solution.py:77
  34.0 1.9 multiply_convert_fusion.1
  35.9 1.8 copy.39
  37.7 0.5 all-to-all-done
  38.2 24.4 %while.12 = (s32[]{:T(128)}, f32[2,512,512]{2,1,0:T(8,128)}, f32[2,512,8]{1,2,0:T(8,128)S(1)}, bf16[2,512,512]{2,1,0:T(8,128)(2,1)}, bf16[192,512]{0,1:T(8,128)(2,1)}, /*index=5*/bf16[192,512]{0,1:T(8,128)(2,1)S(1)}, s32[]{:T(128)}) while((s32[]{:T(128)}, f32[2,512,512]{2,1,0:T(8,128)}, f32[2,512,8]{1,2,0:T(8,128)S(1)}, ...), condition=%wide.region_6.7_spmd, body=%wide.region_4.6_spmd.sunk | while | flops 204468224 | bytes 14598241 | solution.py:108
  38.2 1.9 constant_dynamic-slice_fusion.2
  40.1 2.1 %copy.79 = bf16[1,512,512]{1,2,0:T(8,128)(2,1)} copy(bf16[1,512,512]{2,1,0:T(8,128)(2,1)} %constant_dynamic-slice_fusion.2) | data formatting | bytes 1048576 | tf_op jit(solution)/shard_map/while/body/jit(dynamic_index_in_dim)/dynamic_slice | solution.py:108
  42.1 1.8 fusion.85
  43.9 1.6 fusion.86
  45.6 2.5 %copy.80 = f32[1,512,512]{2,1,0:T(8,128)} copy(f32[1,512,512]{1,2,0:T(8,128)} %bitcast.86) | data formatting | bytes 2097152 | tf_op jit(solution)/shard_map/while/body/jit(dynamic_update_index_in_dim)/dynamic_update_slice | solution.py:108
  48.1 2.3 %constant_dynamic-update-slice_fusion.2 = f32[2,512,512]{2,1,0:T(8,128)} fusion(f32[2,512,512]{2,1,0:T(8,128)} %get-tuple-element.146, f32[1,512,512]{2,1,0:T(8,128)} %copy.80, s32[]{:T(128)S(6)} %copy.86), kind=kLoop, calls=%fused_computation.6.clone.1 | loop fusion | bytes 2097156 | tf_op jit(solution)/shard_map/while/body/jit(dynamic_update_index_in_dim)/dynamic_update_slice | solution.py:108
  50.4 1.9 constant_dynamic-slice_fusion.2
  52.3 2.1 %copy.79 = bf16[1,512,512]{1,2,0:T(8,128)(2,1)} copy(bf16[1,512,512]{2,1,0:T(8,128)(2,1)} %constant_dynamic-slice_fusion.2) | data formatting | bytes 1048576 | tf_op jit(solution)/shard_map/while/body/jit(dynamic_index_in_dim)/dynamic_slice | solution.py:108
  54.3 1.8 fusion.85
  56.1 1.6 fusion.86
  57.8 2.5 %copy.80 = f32[1,512,512]{2,1,0:T(8,128)} copy(f32[1,512,512]{1,2,0:T(8,128)} %bitcast.86) | data formatting | bytes 2097152 | tf_op jit(solution)/shard_map/while/body/jit(dynamic_update_index_in_dim)/dynamic_update_slice | solution.py:108
  60.3 2.3 %constant_dynamic-update-slice_fusion.2 = f32[2,512,512]{2,1,0:T(8,128)} fusion(f32[2,512,512]{2,1,0:T(8,128)} %get-tuple-element.146, f32[1,512,512]{2,1,0:T(8,128)} %copy.80, s32[]{:T(128)S(6)} %copy.86), kind=kLoop, calls=%fused_computation.6.clone.1 | loop fusion | bytes 2097156 | tf_op jit(solution)/shard_map/while/body/jit(dynamic_update_index_in_dim)/dynamic_update_slice | solution.py:108
  62.6 1.0 copy.55
  63.6 2.0 %pad_maximum_fusion = f32[32,32,520]{2,1,0:T(8,128)S(1)} fusion(f32[32,32,8]{2,1,0:T(8,128)} %bitcast.95, f32[32,32,512]{2,1,0:T(8,128)} %bitcast.98), kind=kLoop, calls=%fused_computation.14 | loop fusion | flops 532480 | bytes 4259840 | tf_op jit(solution)/shard_map/concatenate | solution.py:46
  65.7 40.8 %all_to_all.30 = f32[32,32,520]{2,1,0:T(8,128)} all-to-all(f32[32,32,520]{2,1,0:T(8,128)S(1)} %pad_maximum_fusion), channel_id=1, replica_groups=mesh['ba'=8,'aa_0'=4,'aa_1'=4,'aa_2'=2] {'aa_0','aa_1','aa_2'}, dimensions={0} | all-to-all | bytes 4259840 | tf_op jit(solution)/shard_map/all_to_all | solution.py:41
  106.5 1.9 %reduce_sum.130 = f32[32,520]{1,0:T(8,128)S(1)} reduce(f32[32,32,520]{2,1,0:T(8,128)} %all_to_all.30, f32[]{:T(128)} %constant.21.clone.1), dimensions={0}, to_apply=%region_7.8 | reduce | flops 515840 | bytes 2196484 | tf_op jit(solution)/shard_map/reduce_sum | solution.py:42
  108.5 0.7 div.66
  109.3 1.6 multiply_reduce_fusion
  111.0 0.7 fusion.38
  112.6 1.1 broadcast_in_dim.45
  113.7 3.7 %all-to-all-start.2 = ((bf16[16,32,1024]{2,1,0:T(8,128)(2,1)}), bf16[16,32,1024]{2,1,0:T(8,128)(2,1)S(1)}, u32[]{:S(2)}, u32[]{:S(2)}) async-start(bf16[16,32,1024]{2,1,0:T(8,128)(2,1)} %broadcast_in_dim.45), calls=%async_computation.2 | async-start | bytes 2097152 | tf_op jit(solution)/shard_map/all_to_all | solution.py:19
  117.4 17.7 %all-to-all-done.2 = bf16[16,32,1024]{2,1,0:T(8,128)(2,1)S(1)} async-done(((bf16[16,32,1024]{2,1,0:T(8,128)(2,1)}), bf16[16,32,1024]{2,1,0:T(8,128)(2,1)S(1)}, u32[]{:S(2)}, u32[]{:S(2)}) %all-to-all-start.2) | async-done | bytes 1048608 | tf_op jit(solution)/shard_map/all_to_all | solution.py:19
  135.4 6.2 %all_to_all.31 = bf16[2,16,32,1024]{3,2,1,0:T(8,128)(2,1)S(1)} all-to-all(bf16[2,16,32,1024]{3,2,1,0:T(8,128)(2,1)S(1)} %broadcast_in_dim.46), channel_id=1, replica_groups=mesh['ba'=8,'aa_0'=4,'aa_1'=4,'aa_2'=2] {'aa_2'}, dimensions={0} | all-to-all | bytes 4194304 | tf_op jit(solution)/shard_map/all_to_all | solution.py:19
  141.7 1.2 fusion.51
  142.9 1.5 copy.46
  144.4 1.3 copy.45
  146.1 1.8 fusion.20
  148.1 1.6 fusion.34
  149.7 0.5 fusion.41
  150.8 1.1 broadcast_in_dim.47
  151.9 3.7 %all-to-all-start.4 = ((bf16[16,32,1024]{2,1,0:T(8,128)(2,1)}), bf16[16,32,1024]{2,1,0:T(8,128)(2,1)S(1)}, u32[]{:S(2)}, u32[]{:S(2)}) async-start(bf16[16,32,1024]{2,1,0:T(8,128)(2,1)} %broadcast_in_dim.47), calls=%async_computation.4 | async-start | bytes 2097152 | tf_op jit(solution)/shard_map/all_to_all | solution.py:19
  155.6 1.7 fusion.55
  157.9 0.8 copy.53
  158.7 13.2 %all-to-all-done.4 = bf16[16,32,1024]{2,1,0:T(8,128)(2,1)S(1)} async-done(((bf16[16,32,1024]{2,1,0:T(8,128)(2,1)}), bf16[16,32,1024]{2,1,0:T(8,128)(2,1)S(1)}, u32[]{:S(2)}, u32[]{:S(2)}) %all-to-all-start.4) | async-done | bytes 1048608 | tf_op jit(solution)/shard_map/all_to_all | solution.py:19
  172.2 7.4 %all_to_all.32 = bf16[2,16,32,1024]{3,2,1,0:T(8,128)(2,1)S(1)} all-to-all(bf16[2,16,32,1024]{3,2,1,0:T(8,128)(2,1)S(1)} %broadcast_in_dim.48), channel_id=1, replica_groups=mesh['ba'=8,'aa_0'=4,'aa_1'=4,'aa_2'=2] {'aa_2'}, dimensions={0} | all-to-all | bytes 4194304 | tf_op jit(solution)/shard_map/all_to_all | solution.py:19
  179.9 1.2 fusion.50
  181.0 1.5 copy.54
  182.5 1.3 copy.50
  183.9 1.3 fusion.6
  185.2 1.1 fusion.24
  186.4 1.2 fusion.12
  (87 shorter events, 3.8 us)
Async XLA Ops:
  0.6 110.3 %copy-start = (bf16[1024,1536]{1,0:T(8,128)(2,1)S(1)}, bf16[1024,1536]{1,0:T(8,128)(2,1)}, u32[]{:S(2)}) copy-start(bf16[1024,1536]{1,0:T(8,128)(2,1)} %param.18) | copy-start | bytes 9437188
  3.3 17.9 %copy-start.2 = (bf16[192,1024]{1,0:T(8,128)(2,1)S(1)}, bf16[192,1024]{1,0:T(8,128)(2,1)}, u32[]{:S(2)}) copy-start(bf16[192,1024]{1,0:T(8,128)(2,1)} %param.13) | copy-start | bytes 1179652
  12.6 25.6 %all-to-all-start = ((bf16[32,32,512]{2,1,0:T(8,128)(2,1)}), bf16[32,32,512]{2,1,0:T(8,128)(2,1)}, u32[]{:S(2)}, u32[]{:S(2)}) async-start(bf16[32,32,512]{2,1,0:T(8,128)(2,1)} %broadcast_in_dim.44), calls=%async_computation | async-start | bytes 2097152 | tf_op jit(solution)/shard_map/all_to_all | solution.py:19
  21.4 2.2 %copy-start.12 = (f32[192]{0:T(256)}, f32[192]{0:T(256)S(1)}, u32[]{:S(2)}) copy-start(f32[192]{0:T(256)S(1)} %add_rsqrt_fusion.6) | copy-start | bytes 2308
  23.7 0.9 copy-start.5
  24.6 9.5 %copy-start.15 = (f32[1,512]{1,0:T(1,128)S(1)}, f32[1,512]{1,0:T(1,128)}, u32[]{:S(2)}) copy-start(f32[1,512]{1,0:T(1,128)} %get-tuple-element.80) | copy-start | bytes 6148
  26.3 11.9 %copy-start.11 = (f32[2,512,8]{1,2,0:T(8,128)S(1)}, f32[2,512,8]{1,2,0:T(8,128)}, u32[]{:S(2)}) copy-start(f32[2,512,8]{1,2,0:T(8,128)} %custom-call.1) | copy-start | bytes 98308
  106.5 2.8 %copy-start.9 = (bf16[32,1024]{1,0:T(8,128)(2,1)S(1)}, bf16[32,1024]{1,0:T(8,128)(2,1)}, u32[]{:S(2)}) copy-start(bf16[32,1024]{1,0:T(8,128)(2,1)} %param.14) | copy-start | bytes 196612
  110.9 1.6 copy-start.17
  110.9 1.6 copy-start.18
  113.7 21.4 %all-to-all-start.2 = ((bf16[16,32,1024]{2,1,0:T(8,128)(2,1)}), bf16[16,32,1024]{2,1,0:T(8,128)(2,1)S(1)}, u32[]{:S(2)}, u32[]{:S(2)}) async-start(bf16[16,32,1024]{2,1,0:T(8,128)(2,1)} %broadcast_in_dim.45), calls=%async_computation.2 | async-start | bytes 2097152 | tf_op jit(solution)/shard_map/all_to_all | solution.py:19
  145.7 4.0 %copy-start.6 = (bf16[1024,1024]{1,0:T(8,128)(2,1)S(1)}, bf16[1024,1024]{1,0:T(8,128)(2,1)}, u32[]{:S(2)}) copy-start(bf16[1024,1024]{1,0:T(8,128)(2,1)} %param.21) | copy-start | bytes 6291460
  147.9 2.8 %copy-start.16 = (f32[1,512]{1,0:T(1,128)S(1)}, f32[1,512]{1,0:T(1,128)}, u32[]{:S(2)}) copy-start(f32[1,512]{1,0:T(1,128)} %get-tuple-element.82) | copy-start | bytes 6148
  149.7 0.6 copy-start.10
  150.2 5.3 %copy-start.3 = (bf16[192,1024]{1,0:T(8,128)(2,1)S(1)}, bf16[192,1024]{1,0:T(8,128)(2,1)}, u32[]{:S(2)}) copy-start(bf16[192,1024]{1,0:T(8,128)(2,1)} %param.13) | copy-start | bytes 1179652
  150.2 5.4 %copy-start.13 = (f32[192]{0:T(256)S(1)}, f32[192]{0:T(256)}, u32[]{:S(2)}) copy-start(f32[192]{0:T(256)} %copy-done.12) | copy-start | bytes 2308
  151.9 20.0 %all-to-all-start.4 = ((bf16[16,32,1024]{2,1,0:T(8,128)(2,1)}), bf16[16,32,1024]{2,1,0:T(8,128)(2,1)S(1)}, u32[]{:S(2)}, u32[]{:S(2)}) async-start(bf16[16,32,1024]{2,1,0:T(8,128)(2,1)} %broadcast_in_dim.47), calls=%async_computation.4 | async-start | bytes 2097152 | tf_op jit(solution)/shard_map/all_to_all | solution.py:19
  155.6 2.2 %copy-start.14 = (f32[1,512]{1,0:T(1,128)S(1)}, f32[1,512]{1,0:T(1,128)}, u32[]{:S(2)}) copy-start(f32[1,512]{1,0:T(1,128)} %get-tuple-element.77) | copy-start | bytes 6148
  181.0 2.9 %copy-start.7 = (bf16[192,512]{0,1:T(8,128)(2,1)S(1)}, bf16[192,512]{0,1:T(8,128)(2,1)}, u32[]{:S(2)}) copy-start(bf16[192,512]{0,1:T(8,128)(2,1)} %copy.53) | copy-start | bytes 589828
  183.9 1.3 copy-start.4
  185.2 1.2 copy-start.8
  185.2 2.4 %copy-start.1 = (bf16[1024,1536]{1,0:T(8,128)(2,1)S(1)}, bf16[1024,1536]{1,0:T(8,128)(2,1)}, u32[]{:S(2)}) copy-start(bf16[1024,1536]{1,0:T(8,128)(2,1)} %param.18) | copy-start | bytes 9437188
where the time goes:
time: 189 us; the launch traced here: 188 us
  blocking collectives  54.4 us (29%)
  local copies, waits for them, and re-layouts  48.8 us (26%)
  waiting for transfers between devices  31.4 us (17%)
  matrix products  23.2 us (12%)
  starting transfers between devices  15.9 us (8%)
  other arithmetic  12.5 us (7%)
    all_to_all x1, blocking collectives, sent_and_summed(): lax.all_to_all(parts, axis, split_axis=0, concat_axis=0, tiled=True)  40.8 us
    all_to_all x3, waiting for transfers between devices, sent_to_all(): return lax.all_to_all(copies, axis, split_axis=0, concat_axis=0, tiled=True)  31.4 us
    all_to_all x3, starting transfers between devices, sent_to_all(): return lax.all_to_all(copies, axis, split_axis=0, concat_axis=0, tiled=True)  15.9 us
    all_to_all x2, blocking collectives, sent_to_all(): return lax.all_to_all(copies, axis, split_axis=0, concat_axis=0, tiled=True)  13.6 us
    dynamic_update_slice x6, local copies, waits for them, and re-layouts, partial_attend(): lax.map(lambda one_block: attend_block(one_block, key_rows, value_rows, h...  9.7 us
    split x6, local copies, waits for them, and re-layouts, side_by_side_2(): jnp.split(result, [sum(widths[:k]) for k in range(1, len(widths))], axis=...  7.98 us
    dynamic_slice x4, local copies, waits for them, and re-layouts, partial_attend(): lax.map(lambda one_block: attend_block(one_block, key_rows, value_rows, h...  7.86 us
    dot_general x4, matrix products, attend_block(): jnp.einsum('hqk,khe->qhe', weights.astype(jnp.bfloat16), value_heads, pre...  6.23 us
  transfers between devices with their start and end apart: 3, of which 3 were waited for; matrix products, arithmetic and copies ran while one was open for 10% of the time, Pallas kernels for 0%

commit v1 on v0

v1 whole, which is shorter than its diff:
```python
import math

import jax
import jax.numpy as jnp
from jax import lax
from jax.experimental import pallas as pl
from jax.experimental.pallas import tpu as pltpu
from jax.sharding import Mesh
from jax.sharding import PartitionSpec as P

HEADS = 8
AA = ("aa_0", "aa_1", "aa_2")
BA_AA = ("ba", "aa_0", "aa_1", "aa_2")
EPSILON = 1e-06
QUERY_SCALE = math.log2(math.e) / 8.0
F32, BF16 = jnp.float32, jnp.bfloat16


def low_lanes(shape):
    return lax.broadcasted_iota(jnp.int32, shape, len(shape) - 1) % 128 < 64


def swap(x):
    return pltpu.roll(x, 64, axis=1)


def rms_rows(x):
    return (x * lax.rsqrt(jnp.mean(x * x, axis=-1, keepdims=True) + EPSILON)).astype(BF16)


def head_norm(x, gain):
    row = lax.broadcasted_iota(jnp.int32, (256, 256), 0) // 64
    col = lax.broadcasted_iota(jnp.int32, (256, 256), 1) // 64
    averager = jnp.where(row == col, 1.0 / 64, 0.0).astype(BF16)
    squares = (x * x).astype(BF16)
    means = [
        jnp.dot(squares[:, at : at + 256], averager, preferred_element_type=F32)
        for at in range(0, x.shape[1], 256)
    ]
    return x * lax.rsqrt(jnp.concatenate(means, axis=1) + EPSILON) * gain


def matmul(a, b):
    return jnp.dot(a, b, preferred_element_type=F32)


def matmul_t(a, b):
    return lax.dot_general(a, b, (((1,), (1,)), ((), ())), preferred_element_type=F32)


def pair(x, p):
    return x[:, 128 * p : 128 * (p + 1)]


def key_value_heads(keys, values):
    out = []
    for p in range(HEADS // 2):
        k, v = pair(keys, p), pair(values, p)
        low = low_lanes(k.shape)
        out.append(jnp.where(low, k, swap(v)).astype(BF16))
        out.append(jnp.where(low, swap(k), v).astype(BF16))
    return out


def query_heads(queries):
    half = queries.shape[0] // 2
    out = []
    for p in range(HEADS // 2):
        q = pair(queries, p)
        s = swap(q)
        low = low_lanes((half, 128))
        out.append(jnp.where(low, q[:half], s[half:]).astype(BF16))
        out.append(jnp.where(low, s[:half], q[half:]).astype(BF16))
    return out


def with_ones(kv, low):
    return jnp.where(low, jnp.ones_like(kv), kv)


def project_kernel(
    tokens_ref, latents_ref, wq_ref, wkv_ref, wwq_ref, gain_ref, send_ref, keep_ref, give_ref
):
    normed = rms_rows(tokens_ref[...].astype(F32))
    kv = matmul(normed, wkv_ref[...])
    keys = head_norm(kv[:, :512], gain_ref[1:2, :])
    groups = send_ref.shape[0] // HEADS
    count = kv.shape[0] // groups
    for h, block in enumerate(key_value_heads(keys, kv[:, 512:])):
        for g in range(groups):
            send_ref[g * HEADS + h, :count, :] = block[g * count : (g + 1) * count]
    queries = matmul(rms_rows(latents_ref[...].astype(F32)), wq_ref[...])
    queries = head_norm(queries, gain_ref[0:1, :] * QUERY_SCALE)
    for h, block in enumerate(query_heads(queries)):
        for g in range(groups):
            send_ref[g * HEADS + h, count:, :] = block
    writes = head_norm(matmul(normed, wwq_ref[...]), gain_ref[4:5, :] * QUERY_SCALE)
    first = lax.axis_index("aa_2") == 0
    low, high = writes[:, :256], writes[:, 256:]
    keep_ref[...] = jnp.where(first, low, high).astype(BF16)
    give_ref[...] = jnp.where(first, high, low).astype(BF16)


def read_kernel(got_ref, out_ref):
    devices, rows, _ = got_ref.shape
    count = rows - 16
    kv = got_ref[:, :count, :].reshape(devices * count, 128)
    kv1 = with_ones(kv, low_lanes(kv.shape))
    step = 16
    for at in range(0, devices, step):
        packed = got_ref[at : at + step, count:, :].reshape(step * 16, 128).astype(F32)
        low = low_lanes(packed.shape)
        for half, q in enumerate((packed, swap(packed))):
            q = jnp.where(low, q, 0.0).astype(BF16)
            weights = jnp.exp2(matmul_t(q, kv)).astype(BF16)
            o = matmul(weights, kv1)
            out_ref[at : at + step, half * 16 : half * 16 + 16, :] = o.astype(BF16).reshape(
                step, 16, 128
            )


def self_project_kernel(got_ref, latents_ref, wo_ref, wqkv_ref, gain_ref, rows_ref, send_ref):
    devices = got_ref.shape[0]
    groups = devices // HEADS
    blocks = []
    for p in range(HEADS // 2):
        both = []
        for h in (2 * p, 2 * p + 1):
            total = got_ref[h].astype(F32)
            for g in range(1, groups):
                total = total + got_ref[g * HEADS + h].astype(F32)
            both.append(total / swap(total))
        blocks.append(jnp.where(low_lanes(both[0].shape), swap(both[0]), both[1]).astype(BF16))
    attended = jnp.concatenate(blocks, axis=1)
    rows = (latents_ref[...].astype(F32) + matmul(attended, wo_ref[...])).astype(BF16)
    rows_ref[...] = rows
    triple = matmul(rms_rows(rows.astype(F32)), wqkv_ref[...])
    queries = head_norm(triple[:, :512], gain_ref[2:3, :] * QUERY_SCALE)
    keys = head_norm(triple[:, 512:1024], gain_ref[3:4, :])
    count = rows.shape[0]
    kv_blocks = key_value_heads(keys, triple[:, 1024:])
    for h, (kv, q) in enumerate(zip(kv_blocks, query_heads(queries))):
        for g in range(groups):
            send_ref[g * HEADS + h, :count, :] = kv
            send_ref[g * HEADS + h, count:, :] = q


def self_kernel(got_ref, out_ref):
    devices, rows, _ = got_ref.shape
    count = rows - 16
    kv = got_ref[:, :count, :].reshape(devices * count, 128)
    kv1 = with_ones(kv, low_lanes(kv.shape))
    mine = lax.axis_index("aa_0") * HEADS
    packed = got_ref[pl.ds(mine, HEADS), count:, :].reshape(HEADS * 16, 128).astype(F32)
    low = low_lanes(packed.shape)
    outs = []
    for q in (packed, swap(packed)):
        q = jnp.where(low, q, 0.0).astype(BF16)
        weights = jnp.exp2(matmul_t(q, kv)).astype(BF16)
        o = matmul(weights, kv1)
        outs.append(o / swap(o))
    out_ref[...] = jnp.where(low, swap(outs[0]), outs[1]).astype(BF16).reshape(HEADS, 16, 128)


def write_project_kernel(got_ref, rows_ref, wo_ref, wkv_ref, gain_ref, latents_ref, send_ref):
    blocks = []
    for p in range(HEADS // 2):
        e, o = got_ref[2 * p].astype(F32), got_ref[2 * p + 1].astype(F32)
        low = low_lanes(e.shape)
        top, bottom = jnp.where(low, e, swap(o)), jnp.where(low, swap(e), o)
        blocks.append(jnp.concatenate([top, bottom], axis=0).astype(BF16))
    attended = jnp.concatenate(blocks, axis=1)
    rows = (rows_ref[...].astype(F32) + matmul(attended, wo_ref[...])).astype(BF16)
    latents_ref[...] = rows
    kv = matmul(rms_rows(rows.astype(F32)), wkv_ref[...])
    keys, values = head_norm(kv[:, :512], gain_ref[5:6, :]), kv[:, 512:]
    for p in range(HEADS // 2):
        k, v = pair(keys, p), swap(pair(values, p))
        low = low_lanes(k.shape)
        even = jnp.where(low, k, v).astype(BF16)
        odd = jnp.where(low, v, k).astype(BF16)
        core, at = p // 2, 256 * (p % 2)
        for chip in range(send_ref.shape[0] // 2):
            send_ref[2 * chip + core, :, at : at + 128] = even
            send_ref[2 * chip + core, :, at + 128 : at + 256] = odd


def write_kernel(q_ref, got_ref, out_ref):
    devices, rows, _ = got_ref.shape
    for p in range(2):
        q = q_ref[:, 128 * p : 128 * (p + 1)]
        low = low_lanes(q.shape)
        results = []
        for odd in (0, 1):
            at = 128 * (2 * p + odd)
            kv = got_ref[:, :, at : at + 128].reshape(devices * rows, 128)
            keyed = low_lanes(kv.shape)
            if odd:
                keyed, used = jnp.logical_not(keyed), jnp.where(low, jnp.zeros_like(q), q)
            else:
                used = jnp.where(low, q, jnp.zeros_like(q))
            weights = jnp.exp2(matmul_t(used, kv)).astype(BF16)
            o = matmul(weights, with_ones(kv, keyed))
            results.append(o / swap(o))
        even, odd = results
        out_ref[:, 128 * p : 128 * (p + 1)] = swap(jnp.where(low, odd, even)).astype(BF16)


def finish_kernel(tokens_ref, mine_ref, other_ref, wo_ref, out_ref):
    core = lax.axis_index("aa_2")
    own = wo_ref[pl.ds(pl.multiple_of(core * 256, 256), 256), :]
    rest = wo_ref[pl.ds(pl.multiple_of((1 - core) * 256, 256), 256), :]
    update = matmul(mine_ref[...], own) + matmul(other_ref[...], rest)
    out_ref[...] = (tokens_ref[...].astype(F32) + update).astype(BF16)


def call(body, outs, *args, flops=0):
    shapes = tuple(jax.ShapeDtypeStruct(s, BF16) for s in outs)
    return pl.pallas_call(
        body,
        out_shape=shapes if len(shapes) > 1 else shapes[0],
        in_specs=[pl.BlockSpec(memory_space=pltpu.VMEM)] * len(args),
        out_specs=tuple(pl.BlockSpec(memory_space=pltpu.VMEM) for _ in shapes)
        if len(shapes) > 1
        else pl.BlockSpec(memory_space=pltpu.VMEM),
        compiler_params=pltpu.CompilerParams(vmem_limit_bytes=48 * 1024 * 1024),
        cost_estimate=pl.CostEstimate(
            flops=flops,
            transcendentals=0,
            bytes_accessed=sum(a.size * a.dtype.itemsize for a in args),
        ),
    )(*args)


def all_to_all(x, axes):
    return lax.all_to_all(x, axes, split_axis=0, concat_axis=0, tiled=True)


def per_device(
    tokens,
    latents,
    read_query,
    read_keyval,
    read_out,
    self_qkv,
    self_out,
    write_query,
    write_keyval,
    write_out,
    qk_gain,
):
    count, rows = tokens.shape[0], latents.shape[0]
    devices = lax.axis_size(AA)
    groups = devices // HEADS
    other_core = [(0, 1), (1, 0)]
    sent, keep, give = call(
        project_kernel,
        ((devices, count // groups + 16, 128), (count, 256), (count, 256)),
        tokens,
        latents,
        read_query,
        read_keyval,
        write_query,
        qk_gain,
        flops=10**9,
    )
    taken = lax.ppermute(give, "aa_2", other_core)
    got = all_to_all(sent, AA)
    partial = call(read_kernel, ((devices, rows, 128),), got, flops=10**9)
    partial = all_to_all(partial, AA)
    own_rows, sent = call(
        self_project_kernel,
        ((rows, 1024), (devices, rows + 16, 128)),
        partial,
        latents,
        read_out,
        self_qkv,
        qk_gain,
        flops=10**9,
    )
    got = all_to_all(sent, AA)
    attended = call(self_kernel, ((HEADS, 16, 128),), got, flops=10**9)
    attended = all_to_all(attended, ("aa_1", "aa_2"))
    latents_out, sent = call(
        write_project_kernel,
        ((rows, 1024), (devices, rows, 512)),
        attended,
        own_rows,
        self_out,
        write_keyval,
        qk_gain,
        flops=10**9,
    )
    got = all_to_all(sent, AA)
    theirs = call(write_kernel, ((count, 256),), taken, got, flops=10**9)
    other = lax.ppermute(theirs, "aa_2", other_core)
    mine = call(write_kernel, ((count, 256),), keep, got, flops=10**9)
    tokens_out = call(
        finish_kernel, ((count, 1024),), tokens, mine, other, write_out, flops=10**9
    )
    return (tokens_out, latents_out)


def solution(mesh):
    torus = Mesh(mesh.devices.reshape(mesh.shape["ba"], 4, 4, 2), ("ba", "aa_0", "aa_1", "aa_2"))
    in_specs = (P(BA_AA, None), P(BA_AA, None), P(), P(), P(), P(), P(), P(), P(), P(), P())
    out_specs = (P(BA_AA, None), P(BA_AA, None))
    return jax.shard_map(
        per_device, mesh=torus, in_specs=in_specs, out_specs=out_specs, check_vma=False
    )
```

time: 189 us -> 94.3 us (0.50)
  local copies, waits for them, and re-layouts: 48.8 us -> 6.62 us
  matrix products: 23.2 us -> 0 us
  waiting for transfers between devices: 31.4 us -> 16.6 us
  other arithmetic: 12.5 us -> 0 us
  Pallas kernels: 0 us -> 11 us
  starting transfers between devices: 15.9 us -> 4.96 us
    dot_general x16 -> x0, matrix products: 23.2 us -> none  [the longest x4 6.23 us: attend_block(): jnp.einsum('hqk,khe->qhe', weights.astype(jnp.bfloat16), value_heads, pre...]
    all_to_all x3 -> x1, waiting for transfers between devices: 31.4 us -> 15.6 us  [all_to_all(): return lax.all_to_all(x, axes, split_axis=0, concat_axis=0, tiled=True)]
    all_to_all x3 -> x1, starting transfers between devices: 15.9 us -> 4.32 us  [all_to_all(): return lax.all_to_all(x, axes, split_axis=0, concat_axis=0, tiled=True)]
    pallas_call x0 -> x8, Pallas kernels: none -> 11 us  [call(): pl.pallas_call(body, out_shape=shapes if len(shapes) > 1 else shapes[0],...]
    mul x18 -> x0, local copies, waits for them, and re-layouts: 9.99 us -> none  [the longest x12 5.95 us: head_norm(): split_heads * lax.rsqrt(jnp.mean(split_heads * split_heads, axis=-1, keep...]
    dynamic_update_slice x6 -> x0, local copies, waits for them, and re-layouts: 9.7 us -> none  [partial_attend(): lax.map(lambda one_block: attend_block(one_block, key_rows, value_rows, h...]
    split x6 -> x0, local copies, waits for them, and re-layouts: 7.98 us -> none  [side_by_side_2(): jnp.split(result, [sum(widths[:k]) for k in range(1, len(widths))], axis=...]
    dynamic_slice x4 -> x0, local copies, waits for them, and re-layouts: 7.86 us -> none  [partial_attend(): lax.map(lambda one_block: attend_block(one_block, key_rows, value_rows, h...]
  transfers between devices with their start and end apart: 3 -> 3, of which waited for: 3 -> 2; matrix products, arithmetic and copies ran while one was open for 10% -> 0% of each run, Pallas kernels for 0% -> 1%
where the time goes in v1:
time: 94.3 us; the launch traced here: 93.7 us
  blocking collectives  53.8 us (57%)
  waiting for transfers between devices  16.6 us (18%)
  Pallas kernels  11 us (12%)
  local copies, waits for them, and re-layouts  6.62 us (7%)
  starting transfers between devices  4.96 us (5%)
    all_to_all x4, blocking collectives, all_to_all(): return lax.all_to_all(x, axes, split_axis=0, concat_axis=0, tiled=True)  53.8 us
    all_to_all x1, waiting for transfers between devices, all_to_all(): return lax.all_to_all(x, axes, split_axis=0, concat_axis=0, tiled=True)  15.6 us
    pallas_call x8, Pallas kernels, call(): pl.pallas_call(body, out_shape=shapes if len(shapes) > 1 else shapes[0],...  11 us
    unnamed x28, local copies, waits for them, and re-layouts  6.62 us
    all_to_all x1, starting transfers between devices, all_to_all(): return lax.all_to_all(x, axes, split_axis=0, concat_axis=0, tiled=True)  4.32 us
  transfers between devices with their start and end apart: 3, of which 2 were waited for; matrix products, arithmetic and copies ran while one was open for 0% of the time, Pallas kernels for 1%

profile of v1, /device:TPU:1, one launch (start us, length us, event | category | flops | bytes accessed | tf_op | source)
XLA Modules:
  0.0 93.7 jit_solution(11743253622595878128)
XLA Ops:
  0.6 0.0 copy-start.1
  0.6 1.6 %copy-done.1 = bf16[1024,1024]{1,0:T(8,128)(2,1)S(1)} copy-done((bf16[1024,1024]{1,0:T(8,128)(2,1)S(1)}, bf16[1024,1024]{1,0:T(8,128)(2,1)}, u32[]{:S(2)}) %copy-start.1) | copy-done | bytes 2097176
  2.2 0.0 copy-start.3
  2.2 1.2 %copy-done.3 = bf16[1024,512]{1,0:T(8,128)(2,1)S(1)} copy-done((bf16[1024,512]{1,0:T(8,128)(2,1)S(1)}, bf16[1024,512]{1,0:T(8,128)(2,1)}, u32[]{:S(2)}) %copy-start.3) | copy-done | bytes 1048600
  3.4 0.0 copy-start.4
  3.5 1.2 %copy-done.4 = bf16[1024,512]{1,0:T(8,128)(2,1)S(1)} copy-done((bf16[1024,512]{1,0:T(8,128)(2,1)S(1)}, bf16[1024,512]{1,0:T(8,128)(2,1)}, u32[]{:S(2)}) %copy-start.4) | copy-done | bytes 1048600
  4.7 0.0 copy-start.5
  4.7 1.0 %copy-done.5 = bf16[192,1024]{1,0:T(8,128)(2,1)S(1)} copy-done((bf16[192,1024]{1,0:T(8,128)(2,1)S(1)}, bf16[192,1024]{1,0:T(8,128)(2,1)}, u32[]{:S(2)}) %copy-start.5) | copy-done | bytes 393240
  5.7 0.0 copy-start.7
  5.7 0.8 copy-done.7
  6.5 0.0 copy-start.9
  6.5 0.7 copy-done.9
  7.2 1.4 %shard_map.122 = (bf16[32,64,128]{2,1,0:T(8,128)(2,1)S(1)}, bf16[192,256]{1,0:T(8,128)(2,1)S(1)}, bf16[192,256]{1,0:T(8,128)(2,1)S(1)}) custom-call(bf16[192,1024]{1,0:T(8,128)(2,1)S(1)} %copy-done.5, bf16[32,1024]{1,0:T(8,128)(2,1)S(1)} %copy-done.7, bf16[1024,512]{1,0:T(8,128)(2,1)S(1)} %copy-done.3, bf16[1024,1024]{1,0:T(8,128)(2,1)S(1)} %copy-done.1, ...), custom_call_target="tpu_custom_call" | custom-call | flops 1000000000 | bytes 4665344 | tf_op jit(solution)/shard_map/pallas_call | solution.py:219
  8.7 0.0 copy-start.8
  8.7 20.1 %all_to_all.25.got_ref = bf16[32,64,128]{2,1,0:T(8,128)(2,1)S(1)} all-to-all(bf16[32,64,128]{2,1,0:T(8,128)(2,1)S(1)} %get-tuple-element.10), channel_id=1, replica_groups=mesh['ba'=8,'aa_0'=4,'aa_1'=4,'aa_2'=2] {'aa_0','aa_1','aa_2'}, dimensions={0} | all-to-all | bytes 1048576 | tf_op jit(solution)/shard_map/all_to_all | solution.py:236
  28.8 0.0 copy-start
  28.8 0.0 copy-start.2
  28.8 0.0 copy-start.10
  28.8 1.8 %shard_map.123 = bf16[32,32,128]{2,1,0:T(8,128)(2,1)S(1)} custom-call(bf16[32,64,128]{2,1,0:T(8,128)(2,1)S(1)} %all_to_all.25.got_ref), custom_call_target="tpu_custom_call" | custom-call | flops 1000000000 | bytes 524288 | tf_op jit(solution)/shard_map/pallas_call | solution.py:219
  30.6 12.4 %all_to_all.26.got_ref = bf16[32,32,128]{2,1,0:T(8,128)(2,1)S(1)} all-to-all(bf16[32,32,128]{2,1,0:T(8,128)(2,1)S(1)} %shard_map.123), channel_id=1, replica_groups=mesh['ba'=8,'aa_0'=4,'aa_1'=4,'aa_2'=2] {'aa_0','aa_1','aa_2'}, dimensions={0} | all-to-all | bytes 524288 | tf_op jit(solution)/shard_map/all_to_all | solution.py:236
  43.0 0.0 copy-done.8
  43.0 0.0 copy-done
  43.0 0.0 copy-done.2
  43.0 0.0 copy-done.10
  43.0 1.3 %shard_map.124 = (bf16[32,1024]{1,0:T(8,128)(2,1)S(1)}, bf16[32,48,128]{2,1,0:T(8,128)(2,1)S(1)}) custom-call(bf16[32,32,128]{2,1,0:T(8,128)(2,1)S(1)} %all_to_all.26.got_ref, bf16[32,1024]{1,0:T(8,128)(2,1)S(1)} %copy-done.8, bf16[512,1024]{1,0:T(8,128)(2,1)S(1)} %copy-done.2, bf16[1024,1536]{1,0:T(8,128)(2,1)S(1)} %copy-done, f32[6,512]{1,0:T(8,128)S(1)} %copy-done.10), custom_call_target="tpu_custom_call" | custom-call | flops 1000000000 | bytes 4534272 | tf_op jit(solution)/shard_map/pallas_call | solution.py:219
  44.3 0.0 copy-start.11
  44.3 0.0 copy-start.12
  44.3 14.0 %all_to_all.27.got_ref = bf16[32,48,128]{2,1,0:T(8,128)(2,1)S(1)} all-to-all(bf16[32,48,128]{2,1,0:T(8,128)(2,1)S(1)} %get-tuple-element.11), channel_id=1, replica_groups=mesh['ba'=8,'aa_0'=4,'aa_1'=4,'aa_2'=2] {'aa_0','aa_1','aa_2'}, dimensions={0} | all-to-all | bytes 786432 | tf_op jit(solution)/shard_map/all_to_all | solution.py:236
  58.3 0.7 shard_map.125
  59.0 7.3 %all_to_all.28.got_ref = bf16[8,16,128]{2,1,0:T(8,128)(2,1)S(1)} all-to-all(bf16[8,16,128]{2,1,0:T(8,128)(2,1)S(1)} %shard_map.125), channel_id=1, replica_groups=mesh['ba'=8,'aa_0'=4,'aa_1'=4,'aa_2'=2] {'aa_1','aa_2'}, dimensions={0} | all-to-all | bytes 65536 | tf_op jit(solution)/shard_map/all_to_all | solution.py:236
  66.3 0.0 copy-done.11
  66.3 0.0 copy-done.12
  66.3 2.0 %shard_map.126 = (bf16[32,1024]{1,0:T(8,128)(2,1)}, bf16[32,32,512]{2,1,0:T(8,128)(2,1)}) custom-call(bf16[8,16,128]{2,1,0:T(8,128)(2,1)S(1)} %all_to_all.28.got_ref, bf16[32,1024]{1,0:T(8,128)(2,1)S(1)} %get-tuple-element.12.rows_ref, bf16[512,1024]{1,0:T(8,128)(2,1)S(1)} %copy-done.12, bf16[1024,1024]{1,0:T(8,128)(2,1)S(1)} %copy-done.11, ...), custom_call_target="tpu_custom_call" | custom-call | flops 1000000000 | bytes 3256320 | tf_op jit(solution)/shard_map/pallas_call | solution.py:219
  68.3 4.3 %all-to-all-start.4 = ((bf16[32,32,512]{2,1,0:T(8,128)(2,1)}), bf16[32,32,512]{2,1,0:T(8,128)(2,1)S(1)}, u32[]{:S(2)}, u32[]{:S(2)}) async-start(bf16[32,32,512]{2,1,0:T(8,128)(2,1)} %get-tuple-element.13), calls=%async_computation.4 | async-start | bytes 2097152 | tf_op jit(solution)/shard_map/all_to_all | solution.py:236
  72.6 0.4 collective-permute-start
  73.1 1.0 %collective-permute-done.q_ref = bf16[192,256]{1,0:T(8,128)(2,1)S(1)} collective-permute-done((bf16[192,256]{1,0:T(8,128)(2,1)S(1)}, bf16[192,256]{1,0:T(8,128)(2,1)S(1)}, u32[]{:S(2)}, u32[]{:S(2)}) %collective-permute-start) | collective-permute-done | bytes 98336 | tf_op jit(solution)/shard_map/ppermute | solution.py:267
  74.0 15.6 %all-to-all-done.4.got_ref = bf16[32,32,512]{2,1,0:T(8,128)(2,1)S(1)} async-done(((bf16[32,32,512]{2,1,0:T(8,128)(2,1)}), bf16[32,32,512]{2,1,0:T(8,128)(2,1)S(1)}, u32[]{:S(2)}, u32[]{:S(2)}) %all-to-all-start.4) | async-done | bytes 1048608 | tf_op jit(solution)/shard_map/all_to_all | solution.py:236
  89.6 1.3 %shard_map.128 = bf16[192,256]{1,0:T(8,128)(2,1)S(1)} custom-call(bf16[192,256]{1,0:T(8,128)(2,1)S(1)} %collective-permute-done.q_ref, bf16[32,32,512]{2,1,0:T(8,128)(2,1)S(1)} %all-to-all-done.4.got_ref), custom_call_target="tpu_custom_call" | custom-call | flops 1000000000 | bytes 1146880 | tf_op jit(solution)/shard_map/pallas_call | solution.py:219
  91.0 0.0 copy-start.6
  91.0 0.0 copy-start.13
  91.0 0.2 collective-permute-start.1
  91.2 1.3 %shard_map.127.mine_ref = bf16[192,256]{1,0:T(8,128)(2,1)S(1)} custom-call(bf16[192,256]{1,0:T(8,128)(2,1)S(1)} %get-tuple-element.9.q_ref, bf16[32,32,512]{2,1,0:T(8,128)(2,1)S(1)} %all-to-all-done.4.got_ref), custom_call_target="tpu_custom_call" | custom-call | flops 1000000000 | bytes 1146880 | tf_op jit(solution)/shard_map/pallas_call | solution.py:219
  92.5 0.0 collective-permute-done.1.other_ref
  92.5 0.0 copy-done.6
  92.5 0.0 copy-done.13
  92.5 1.1 %shard_map.129 = bf16[192,1024]{1,0:T(8,128)(2,1)} custom-call(bf16[192,1024]{1,0:T(8,128)(2,1)S(1)} %copy-done.6, bf16[192,256]{1,0:T(8,128)(2,1)S(1)} %shard_map.127.mine_ref, bf16[192,256]{1,0:T(8,128)(2,1)S(1)} %collective-permute-done.1.other_ref, bf16[512,1024]{1,0:T(8,128)(2,1)S(1)} %copy-done.13), custom_call_target="tpu_custom_call" | custom-call | flops 1000000000 | bytes 1638400 | tf_op jit(solution)/shard_map/pallas_call | solution.py:219
Async XLA Ops:
  0.6 1.6 %copy-start.1 = (bf16[1024,1024]{1,0:T(8,128)(2,1)S(1)}, bf16[1024,1024]{1,0:T(8,128)(2,1)}, u32[]{:S(2)}) copy-start(bf16[1024,1024]{1,0:T(8,128)(2,1)} %wkv_ref.2) | copy-start | bytes 6291460
  2.2 1.2 %copy-start.3 = (bf16[1024,512]{1,0:T(8,128)(2,1)S(1)}, bf16[1024,512]{1,0:T(8,128)(2,1)}, u32[]{:S(2)}) copy-start(bf16[1024,512]{1,0:T(8,128)(2,1)} %wq_ref.1) | copy-start | bytes 3145732
  3.4 1.2 %copy-start.4 = (bf16[1024,512]{1,0:T(8,128)(2,1)S(1)}, bf16[1024,512]{1,0:T(8,128)(2,1)}, u32[]{:S(2)}) copy-start(bf16[1024,512]{1,0:T(8,128)(2,1)} %wwq_ref.1) | copy-start | bytes 3145732
  4.7 1.0 %copy-start.5 = (bf16[192,1024]{1,0:T(8,128)(2,1)S(1)}, bf16[192,1024]{1,0:T(8,128)(2,1)}, u32[]{:S(2)}) copy-start(bf16[192,1024]{1,0:T(8,128)(2,1)} %tokens_ref.3) | copy-start | bytes 1179652
  5.7 0.8 copy-start.7
  6.5 0.7 copy-start.9
  8.7 34.3 %copy-start.8 = (bf16[32,1024]{1,0:T(8,128)(2,1)S(1)}, bf16[32,1024]{1,0:T(8,128)(2,1)}, u32[]{:S(2)}) copy-start(bf16[32,1024]{1,0:T(8,128)(2,1)} %latents_ref.3) | copy-start | bytes 196612
  28.8 14.2 %copy-start = (bf16[1024,1536]{1,0:T(8,128)(2,1)S(1)}, bf16[1024,1536]{1,0:T(8,128)(2,1)}, u32[]{:S(2)}) copy-start(bf16[1024,1536]{1,0:T(8,128)(2,1)} %wqkv_ref.1) | copy-start | bytes 9437188
  28.8 14.2 %copy-start.2 = (bf16[512,1024]{1,0:T(8,128)(2,1)S(1)}, bf16[512,1024]{1,0:T(8,128)(2,1)}, u32[]{:S(2)}) copy-start(bf16[512,1024]{1,0:T(8,128)(2,1)} %wo_ref.3) | copy-start | bytes 3145732
  28.8 14.2 %copy-start.10 = (f32[6,512]{1,0:T(8,128)S(1)}, f32[6,512]{1,0:T(8,128)}, u32[]{:S(2)}) copy-start(f32[6,512]{1,0:T(8,128)} %gain_ref.5) | copy-start | bytes 36868
  44.3 22.0 %copy-start.11 = (bf16[1024,1024]{1,0:T(8,128)(2,1)S(1)}, bf16[1024,1024]{1,0:T(8,128)(2,1)}, u32[]{:S(2)}) copy-start(bf16[1024,1024]{1,0:T(8,128)(2,1)} %wkv_ref.3) | copy-start | bytes 6291460
  44.3 22.0 %copy-start.12 = (bf16[512,1024]{1,0:T(8,128)(2,1)S(1)}, bf16[512,1024]{1,0:T(8,128)(2,1)}, u32[]{:S(2)}) copy-start(bf16[512,1024]{1,0:T(8,128)(2,1)} %wo_ref.4) | copy-start | bytes 3145732
  68.3 21.3 %all-to-all-start.4 = ((bf16[32,32,512]{2,1,0:T(8,128)(2,1)}), bf16[32,32,512]{2,1,0:T(8,128)(2,1)S(1)}, u32[]{:S(2)}, u32[]{:S(2)}) async-start(bf16[32,32,512]{2,1,0:T(8,128)(2,1)} %get-tuple-element.13), calls=%async_computation.4 | async-start | bytes 2097152 | tf_op jit(solution)/shard_map/all_to_all | solution.py:236
  72.6 1.4 %collective-permute-start = (bf16[192,256]{1,0:T(8,128)(2,1)S(1)}, bf16[192,256]{1,0:T(8,128)(2,1)S(1)}, u32[]{:S(2)}, u32[]{:S(2)}) collective-permute-start(bf16[192,256]{1,0:T(8,128)(2,1)S(1)} %get-tuple-element.14), channel_id=1, source_target_pairs={{0,1},{1,0},{2,3},{3,2},{4,5},{5,4},{6,7},{7,6},{8,9},{9,8},{10,11... | collective-permute-start | bytes 294920 | tf_op jit(solution)/shard_map/ppermute | solution.py:267
  91.0 1.6 %copy-start.6 = (bf16[192,1024]{1,0:T(8,128)(2,1)S(1)}, bf16[192,1024]{1,0:T(8,128)(2,1)}, u32[]{:S(2)}) copy-start(bf16[192,1024]{1,0:T(8,128)(2,1)} %tokens_ref.3) | copy-start | bytes 1179652
  91.0 1.6 %copy-start.13 = (bf16[512,1024]{1,0:T(8,128)(2,1)S(1)}, bf16[512,1024]{1,0:T(8,128)(2,1)}, u32[]{:S(2)}) copy-start(bf16[512,1024]{1,0:T(8,128)(2,1)} %wo_ref.5) | copy-start | bytes 3145732
  91.0 1.5 %collective-permute-start.1 = (bf16[192,256]{1,0:T(8,128)(2,1)S(1)}, bf16[192,256]{1,0:T(8,128)(2,1)S(1)}, u32[]{:S(2)}, u32[]{:S(2)}) collective-permute-start(bf16[192,256]{1,0:T(8,128)(2,1)S(1)} %shard_map.128), channel_id=1, source_target_pairs={{0,1},{1,0},{2,3},{3,2},{4,5},{5,4},{6,7},{7,6},{8,9},{9,8},{10,11... | collective-permute-start | bytes 294920 | tf_op jit(solution)/shard_map/ppermute | solution.py:296

commit v2 on v1

--- a/solution.py
+++ b/solution.py
@@ -79,21 +79,58 @@
 
 
 def project_kernel(
-    tokens_ref, latents_ref, wq_ref, wkv_ref, wwq_ref, gain_ref, send_ref, keep_ref, give_ref
+    tokens_hbm,
+    latents_hbm,
+    wq_hbm,
+    wkv_hbm,
+    gain_hbm,
+    send_ref,
+    tokens_ref,
+    latents_ref,
+    wq_ref,
+    wkv_ref,
+    gain_ref,
+    sems,
 ):
+    half = wkv_ref.shape[1] // 2
+    copies = [
+        pltpu.make_async_copy(src, dst, sems.at[i])
+        for i, (src, dst) in enumerate(
+            (
+                (gain_hbm, gain_ref),
+                (latents_hbm, latents_ref),
+                (tokens_hbm, tokens_ref),
+                (wq_hbm, wq_ref),
+                (wkv_hbm.at[:, :half], wkv_ref.at[:, :half]),
+                (wkv_hbm.at[:, half:], wkv_ref.at[:, half:]),
+            )
+        )
+    ]
+    for copy in copies:
+        copy.start()
+    groups = send_ref.shape[0] // HEADS
+    count = tokens_ref.shape[0] // groups
+    copies[0].wait()
+    copies[1].wait()
+    latents = rms_rows(latents_ref[...].astype(F32))
+    copies[2].wait()
     normed = rms_rows(tokens_ref[...].astype(F32))
-    kv = matmul(normed, wkv_ref[...])
-    keys = head_norm(kv[:, :512], gain_ref[1:2, :])
-    groups = send_ref.shape[0] // HEADS
-    count = kv.shape[0] // groups
-    for h, block in enumerate(key_value_heads(keys, kv[:, 512:])):
-        for g in range(groups):
-            send_ref[g * HEADS + h, :count, :] = block[g * count : (g + 1) * count]
-    queries = matmul(rms_rows(latents_ref[...].astype(F32)), wq_ref[...])
-    queries = head_norm(queries, gain_ref[0:1, :] * QUERY_SCALE)
+    copies[3].wait()
+    queries = head_norm(matmul(latents, wq_ref[...]), gain_ref[0:1, :] * QUERY_SCALE)
     for h, block in enumerate(query_heads(queries)):
         for g in range(groups):
             send_ref[g * HEADS + h, count:, :] = block
+    copies[4].wait()
+    keys = head_norm(matmul(normed, wkv_ref[:, :half]), gain_ref[1:2, :])
+    copies[5].wait()
+    values = matmul(normed, wkv_ref[:, half:])
+    for h, block in enumerate(key_value_heads(keys, values)):
+        for g in range(groups):
+            send_ref[g * HEADS + h, :count, :] = block[g * count : (g + 1) * count]
+
+
+def write_query_kernel(tokens_ref, wwq_ref, gain_ref, keep_ref, give_ref):
+    normed = rms_rows(tokens_ref[...].astype(F32))
     writes = head_norm(matmul(normed, wwq_ref[...]), gain_ref[4:5, :] * QUERY_SCALE)
     first = lax.axis_index("aa_2") == 0
     low, high = writes[:, :256], writes[:, 256:]
@@ -214,12 +251,18 @@
     out_ref[...] = (tokens_ref[...].astype(F32) + update).astype(BF16)
 
 
-def call(body, outs, *args, flops=0):
+def call(body, outs, *args, flops=0, fetch=False):
+    space = pltpu.HBM if fetch else pltpu.VMEM
+    scratch = [pltpu.VMEM(a.shape, a.dtype) for a in args] if fetch else []
+    if fetch:
+        scratch.append(pltpu.SemaphoreType.DMA((len(args) + 1,)))
+        args = [pltpu.with_memory_space_constraint(a, space) for a in args]
     shapes = tuple(jax.ShapeDtypeStruct(s, BF16) for s in outs)
     return pl.pallas_call(
         body,
         out_shape=shapes if len(shapes) > 1 else shapes[0],
-        in_specs=[pl.BlockSpec(memory_space=pltpu.VMEM)] * len(args),
+        in_specs=[pl.BlockSpec(memory_space=space)] * len(args),
+        scratch_shapes=scratch,
         out_specs=tuple(pl.BlockSpec(memory_space=pltpu.VMEM) for _ in shapes)
         if len(shapes) > 1
         else pl.BlockSpec(memory_space=pltpu.VMEM),
@@ -253,18 +296,17 @@
     devices = lax.axis_size(AA)
     groups = devices // HEADS
     other_core = [(0, 1), (1, 0)]
-    sent, keep, give = call(
+    sent = call(
         project_kernel,
-        ((devices, count // groups + 16, 128), (count, 256), (count, 256)),
+        ((devices, count // groups + 16, 128),),
         tokens,
         latents,
         read_query,
         read_keyval,
-        write_query,
         qk_gain,
         flops=10**9,
-    )
-    taken = lax.ppermute(give, "aa_2", other_core)
+        fetch=True,
+    )
     got = all_to_all(sent, AA)
     partial = call(read_kernel, ((devices, rows, 128),), got, flops=10**9)
     partial = all_to_all(partial, AA)
@@ -292,6 +334,15 @@
         flops=10**9,
     )
     got = all_to_all(sent, AA)
+    keep, give = call(
+        write_query_kernel,
+        ((count, 256), (count, 256)),
+        tokens,
+        write_query,
+        qk_gain,
+        flops=10**9,
+    )
+    taken = lax.ppermute(give, "aa_2", other_core)
     theirs = call(write_kernel, ((count, 256),), taken, got, flops=10**9)
     other = lax.ppermute(theirs, "aa_2", other_core)
     mine = call(write_kernel, ((count, 256),), keep, got, flops=10**9)

time: 94.3 us -> 88.9 us (0.943)
  local copies, waits for them, and re-layouts: 6.62 us -> 0.04 us
  Pallas kernels: 11 us -> 13.1 us
    unnamed x28 -> x18, local copies, waits for them, and re-layouts: 6.62 us -> 0.04 us
    pallas_call x8 -> x9, Pallas kernels: 11 us -> 13.1 us  [call(): pl.pallas_call(body, out_shape=shapes if len(shapes) > 1 else shapes[0],...]
  transfers between devices with their start and end apart: 3 -> 3, of which waited for: 2 -> 2; matrix products, arithmetic and copies ran while one was open for 0% -> 0% of each run, Pallas kernels for 1% -> 2%
where the time goes in v2:
time: 88.9 us; the launch traced here: 88.6 us
  blocking collectives  53.8 us (61%)
  waiting for transfers between devices  15.9 us (18%)
  Pallas kernels  13.1 us (15%)
  starting transfers between devices  4.97 us (6%)
    all_to_all x4, blocking collectives, all_to_all(): return lax.all_to_all(x, axes, split_axis=0, concat_axis=0, tiled=True)  53.8 us
    all_to_all x1, waiting for transfers between devices, all_to_all(): return lax.all_to_all(x, axes, split_axis=0, concat_axis=0, tiled=True)  15 us
    pallas_call x9, Pallas kernels, call(): pl.pallas_call(body, out_shape=shapes if len(shapes) > 1 else shapes[0],...  13.1 us
    all_to_all x1, starting transfers between devices, all_to_all(): return lax.all_to_all(x, axes, split_axis=0, concat_axis=0, tiled=True)  4.31 us
  transfers between devices with their start and end apart: 3, of which 2 were waited for; matrix products, arithmetic and copies ran while one was open for 0% of the time, Pallas kernels for 2%

profile of v2, /device:TPU:1, one launch (start us, length us, event | category | flops | bytes accessed | tf_op | source)
XLA Modules:
  0.0 88.6 jit_solution(5549366711034710215)
XLA Ops:
  0.6 2.9 %shard_map.123 = bf16[32,64,128]{2,1,0:T(8,128)(2,1)S(1)} custom-call(bf16[192,1024]{1,0:T(8,128)(2,1)} %tokens_ref.3, bf16[32,1024]{1,0:T(8,128)(2,1)} %latents_ref.1, bf16[1024,512]{1,0:T(8,128)(2,1)} %wq_hbm.1, bf16[1024,1024]{1,0:T(8,128)(2,1)} %wkv_hbm.1, f32[6,512]{1,0:T(8,128)} %gain_ref.5), custom_call_target="tpu_custom_call" | custom-call | flops 1000000000 | bytes 3616768 | tf_op jit(solution)/shard_map/pallas_call | solution.py:261
  3.6 0.0 copy-start.3
  3.6 20.1 %all_to_all.25.got_ref = bf16[32,64,128]{2,1,0:T(8,128)(2,1)S(1)} all-to-all(bf16[32,64,128]{2,1,0:T(8,128)(2,1)S(1)} %shard_map.123), channel_id=1, replica_groups=mesh['ba'=8,'aa_0'=4,'aa_1'=4,'aa_2'=2] {'aa_0','aa_1','aa_2'}, dimensions={0} | all-to-all | bytes 1048576 | tf_op jit(solution)/shard_map/all_to_all | solution.py:279
  23.7 0.0 copy-start
  23.7 0.0 copy-start.1
  23.7 0.0 copy-start.4
  23.7 1.8 %shard_map.124 = bf16[32,32,128]{2,1,0:T(8,128)(2,1)S(1)} custom-call(bf16[32,64,128]{2,1,0:T(8,128)(2,1)S(1)} %all_to_all.25.got_ref), custom_call_target="tpu_custom_call" | custom-call | flops 1000000000 | bytes 524288 | tf_op jit(solution)/shard_map/pallas_call | solution.py:261
  25.5 12.4 %all_to_all.26.got_ref = bf16[32,32,128]{2,1,0:T(8,128)(2,1)S(1)} all-to-all(bf16[32,32,128]{2,1,0:T(8,128)(2,1)S(1)} %shard_map.124), channel_id=1, replica_groups=mesh['ba'=8,'aa_0'=4,'aa_1'=4,'aa_2'=2] {'aa_0','aa_1','aa_2'}, dimensions={0} | all-to-all | bytes 524288 | tf_op jit(solution)/shard_map/all_to_all | solution.py:279
  37.9 0.0 copy-done.3
  37.9 0.0 copy-done
  37.9 0.0 copy-done.1
  37.9 0.0 copy-done.4
  37.9 1.3 %shard_map.125 = (bf16[32,1024]{1,0:T(8,128)(2,1)S(1)}, bf16[32,48,128]{2,1,0:T(8,128)(2,1)S(1)}) custom-call(bf16[32,32,128]{2,1,0:T(8,128)(2,1)S(1)} %all_to_all.26.got_ref, bf16[32,1024]{1,0:T(8,128)(2,1)S(1)} %copy-done.3, bf16[512,1024]{1,0:T(8,128)(2,1)S(1)} %copy-done.1, bf16[1024,1536]{1,0:T(8,128)(2,1)S(1)} %copy-done, f32[6,512]{1,0:T(8,128)S(1)} %copy-done.4), custom_call_target="tpu_custom_call" | custom-call | flops 1000000000 | bytes 4534272 | tf_op jit(solution)/shard_map/pallas_call | solution.py:261
  39.2 0.0 copy-start.5
  39.2 0.0 copy-start.6
  39.2 14.0 %all_to_all.27.got_ref = bf16[32,48,128]{2,1,0:T(8,128)(2,1)S(1)} all-to-all(bf16[32,48,128]{2,1,0:T(8,128)(2,1)S(1)} %get-tuple-element.9), channel_id=1, replica_groups=mesh['ba'=8,'aa_0'=4,'aa_1'=4,'aa_2'=2] {'aa_0','aa_1','aa_2'}, dimensions={0} | all-to-all | bytes 786432 | tf_op jit(solution)/shard_map/all_to_all | solution.py:279
  53.2 0.7 shard_map.126
  53.9 7.3 %all_to_all.28.got_ref = bf16[8,16,128]{2,1,0:T(8,128)(2,1)S(1)} all-to-all(bf16[8,16,128]{2,1,0:T(8,128)(2,1)S(1)} %shard_map.126), channel_id=1, replica_groups=mesh['ba'=8,'aa_0'=4,'aa_1'=4,'aa_2'=2] {'aa_1','aa_2'}, dimensions={0} | all-to-all | bytes 65536 | tf_op jit(solution)/shard_map/all_to_all | solution.py:279
  61.2 0.0 copy-done.5
  61.2 0.0 copy-done.6
  61.2 0.0 copy-start.2
  61.2 0.0 copy-start.7
  61.2 2.0 %shard_map.127 = (bf16[32,1024]{1,0:T(8,128)(2,1)}, bf16[32,32,512]{2,1,0:T(8,128)(2,1)}) custom-call(bf16[8,16,128]{2,1,0:T(8,128)(2,1)S(1)} %all_to_all.28.got_ref, bf16[32,1024]{1,0:T(8,128)(2,1)S(1)} %get-tuple-element.10.rows_ref, bf16[512,1024]{1,0:T(8,128)(2,1)S(1)} %copy-done.6, bf16[1024,1024]{1,0:T(8,128)(2,1)S(1)} %copy-done.5, f32[6,512]{1,0:T(8,128)S(1)} %copy-done.4), custom_call_target="tpu_custom_call" | custom-call | flops 1000000000 | bytes 3256320 | tf_op jit(solution)/shard_map/pallas_call | solution.py:261
  63.2 4.3 %all-to-all-start.4 = ((bf16[32,32,512]{2,1,0:T(8,128)(2,1)}), bf16[32,32,512]{2,1,0:T(8,128)(2,1)S(1)}, u32[]{:S(2)}, u32[]{:S(2)}) async-start(bf16[32,32,512]{2,1,0:T(8,128)(2,1)} %get-tuple-element.11), calls=%async_computation.4 | async-start | bytes 2097152 | tf_op jit(solution)/shard_map/all_to_all | solution.py:279
  67.5 0.0 copy-done.2
  67.6 0.0 copy-done.7
  67.6 0.6 shard_map.122
  68.2 0.4 collective-permute-start
  68.6 0.9 %collective-permute-done.q_ref = bf16[192,256]{1,0:T(8,128)(2,1)S(1)} collective-permute-done((bf16[192,256]{1,0:T(8,128)(2,1)S(1)}, bf16[192,256]{1,0:T(8,128)(2,1)S(1)}, u32[]{:S(2)}, u32[]{:S(2)}) %collective-permute-start) | collective-permute-done | bytes 98336 | tf_op jit(solution)/shard_map/ppermute | solution.py:345
  69.6 15.0 %all-to-all-done.4.got_ref = bf16[32,32,512]{2,1,0:T(8,128)(2,1)S(1)} async-done(((bf16[32,32,512]{2,1,0:T(8,128)(2,1)}), bf16[32,32,512]{2,1,0:T(8,128)(2,1)S(1)}, u32[]{:S(2)}, u32[]{:S(2)}) %all-to-all-start.4) | async-done | bytes 1048608 | tf_op jit(solution)/shard_map/all_to_all | solution.py:279
  84.5 1.3 %shard_map.129 = bf16[192,256]{1,0:T(8,128)(2,1)S(1)} custom-call(bf16[192,256]{1,0:T(8,128)(2,1)S(1)} %collective-permute-done.q_ref, bf16[32,32,512]{2,1,0:T(8,128)(2,1)S(1)} %all-to-all-done.4.got_ref), custom_call_target="tpu_custom_call" | custom-call | flops 1000000000 | bytes 1146880 | tf_op jit(solution)/shard_map/pallas_call | solution.py:261
  85.9 0.0 copy-start.8
  85.9 0.2 collective-permute-start.1
  86.1 1.3 %shard_map.128.mine_ref = bf16[192,256]{1,0:T(8,128)(2,1)S(1)} custom-call(bf16[192,256]{1,0:T(8,128)(2,1)S(1)} %get-tuple-element.8.q_ref, bf16[32,32,512]{2,1,0:T(8,128)(2,1)S(1)} %all-to-all-done.4.got_ref), custom_call_target="tpu_custom_call" | custom-call | flops 1000000000 | bytes 1146880 | tf_op jit(solution)/shard_map/pallas_call | solution.py:261
  87.4 0.0 collective-permute-done.1.other_ref
  87.4 0.0 copy-done.8
  87.4 1.2 %shard_map.130 = bf16[192,1024]{1,0:T(8,128)(2,1)} custom-call(bf16[192,1024]{1,0:T(8,128)(2,1)S(1)} %copy-done.2, bf16[192,256]{1,0:T(8,128)(2,1)S(1)} %shard_map.128.mine_ref, bf16[192,256]{1,0:T(8,128)(2,1)S(1)} %collective-permute-done.1.other_ref, bf16[512,1024]{1,0:T(8,128)(2,1)S(1)} %copy-done.8), custom_call_target="tpu_custom_call" | custom-call | flops 1000000000 | bytes 1638400 | tf_op jit(solution)/shard_map/pallas_call | solution.py:261
Async XLA Ops:
  3.6 34.3 %copy-start.3 = (bf16[32,1024]{1,0:T(8,128)(2,1)S(1)}, bf16[32,1024]{1,0:T(8,128)(2,1)}, u32[]{:S(2)}) copy-start(bf16[32,1024]{1,0:T(8,128)(2,1)} %latents_ref.1) | copy-start | bytes 196612
  23.7 14.2 %copy-start = (bf16[1024,1536]{1,0:T(8,128)(2,1)S(1)}, bf16[1024,1536]{1,0:T(8,128)(2,1)}, u32[]{:S(2)}) copy-start(bf16[1024,1536]{1,0:T(8,128)(2,1)} %wqkv_ref.1) | copy-start | bytes 9437188
  23.7 14.2 %copy-start.1 = (bf16[512,1024]{1,0:T(8,128)(2,1)S(1)}, bf16[512,1024]{1,0:T(8,128)(2,1)}, u32[]{:S(2)}) copy-start(bf16[512,1024]{1,0:T(8,128)(2,1)} %wo_ref.3) | copy-start | bytes 3145732
  23.7 14.2 %copy-start.4 = (f32[6,512]{1,0:T(8,128)S(1)}, f32[6,512]{1,0:T(8,128)}, u32[]{:S(2)}) copy-start(f32[6,512]{1,0:T(8,128)} %gain_ref.5) | copy-start | bytes 36868
  39.2 22.0 %copy-start.5 = (bf16[1024,1024]{1,0:T(8,128)(2,1)S(1)}, bf16[1024,1024]{1,0:T(8,128)(2,1)}, u32[]{:S(2)}) copy-start(bf16[1024,1024]{1,0:T(8,128)(2,1)} %wkv_ref.1) | copy-start | bytes 6291460
  39.2 22.0 %copy-start.6 = (bf16[512,1024]{1,0:T(8,128)(2,1)S(1)}, bf16[512,1024]{1,0:T(8,128)(2,1)}, u32[]{:S(2)}) copy-start(bf16[512,1024]{1,0:T(8,128)(2,1)} %wo_ref.4) | copy-start | bytes 3145732
  61.2 6.3 %copy-start.2 = (bf16[192,1024]{1,0:T(8,128)(2,1)S(1)}, bf16[192,1024]{1,0:T(8,128)(2,1)}, u32[]{:S(2)}) copy-start(bf16[192,1024]{1,0:T(8,128)(2,1)} %tokens_ref.3) | copy-start | bytes 1179652
  61.2 6.3 %copy-start.7 = (bf16[1024,512]{1,0:T(8,128)(2,1)S(1)}, bf16[1024,512]{1,0:T(8,128)(2,1)}, u32[]{:S(2)}) copy-start(bf16[1024,512]{1,0:T(8,128)(2,1)} %wwq_ref.1) | copy-start | bytes 3145732
  63.2 21.3 %all-to-all-start.4 = ((bf16[32,32,512]{2,1,0:T(8,128)(2,1)}), bf16[32,32,512]{2,1,0:T(8,128)(2,1)S(1)}, u32[]{:S(2)}, u32[]{:S(2)}) async-start(bf16[32,32,512]{2,1,0:T(8,128)(2,1)} %get-tuple-element.11), calls=%async_computation.4 | async-start | bytes 2097152 | tf_op jit(solution)/shard_map/all_to_all | solution.py:279
  68.2 1.4 %collective-permute-start = (bf16[192,256]{1,0:T(8,128)(2,1)S(1)}, bf16[192,256]{1,0:T(8,128)(2,1)S(1)}, u32[]{:S(2)}, u32[]{:S(2)}) collective-permute-start(bf16[192,256]{1,0:T(8,128)(2,1)S(1)} %get-tuple-element.12), channel_id=1, source_target_pairs={{0,1},{1,0},{2,3},{3,2},{4,5},{5,4},{6,7},{7,6},{8,9},{9,8},{10,11... | collective-permute-start | bytes 294920 | tf_op jit(solution)/shard_map/ppermute | solution.py:345
  85.9 1.6 %copy-start.8 = (bf16[512,1024]{1,0:T(8,128)(2,1)S(1)}, bf16[512,1024]{1,0:T(8,128)(2,1)}, u32[]{:S(2)}) copy-start(bf16[512,1024]{1,0:T(8,128)(2,1)} %wo_ref.5) | copy-start | bytes 3145732
  85.9 1.5 %collective-permute-start.1 = (bf16[192,256]{1,0:T(8,128)(2,1)S(1)}, bf16[192,256]{1,0:T(8,128)(2,1)S(1)}, u32[]{:S(2)}, u32[]{:S(2)}) collective-permute-start(bf16[192,256]{1,0:T(8,128)(2,1)S(1)} %shard_map.129), channel_id=1, source_target_pairs={{0,1},{1,0},{2,3},{3,2},{4,5},{5,4},{6,7},{7,6},{8,9},{9,8},{10,11... | collective-permute-start | bytes 294920 | tf_op jit(solution)/shard_map/ppermute | solution.py:347
